TPU v7x, 32 devices: a whole 2x2x4 slice. The times are simulated.
32 devices in a mesh: rep: 16 (over z, y, core), tp: 2 (over x).
Axes of the slice: x: 2, y: 2, z: 4, core: 2. Of those that a mesh axis runs over, the one named last changes fastest.
Arguments:
- activations: bfloat16 [8192, 6144], P('rep', 'tp'), may hold values from -6 to 6
- norm_gain: float32 [6144], replicated, may hold values from 0.5 to 1.5
- query_gain: float32 [128], replicated, may hold values from 0.5 to 18
- key_gain: float32 [128], replicated, may hold values from 0.5 to 18
- project_in: bfloat16 [6144, 24, 384], P('rep', 'tp'), may hold values from -1 to 1
- project_out: bfloat16 [6144, 3072], P('rep', 'tp'), may hold values from -1 to 1
Outputs:
- attended: bfloat16 [8192, 6144], P('rep', 'tp')
- weight_norms: float32 [2], replicated
All inputs are finite; a program needn't handle non-finite values.
Results may differ from a plain program's by a relative error of at most 0.018.
The roundings to bfloat16 on the way count: a program that leaves them out, or rounds other values in their place, can miss the bound.
Values may be sent and summed in bfloat16 or wider, within the bound.
A program may use at most 192 MiB of HBM per device.

v0:
```python
import math
import jax
import jax.numpy as jnp
from jax import lax
from jax.sharding import PartitionSpec as P

D = 6144
HEADS = 24
HEAD_DIM = 128
PATCHES = 256


def layer_norm(values, gain):
    average = jnp.mean(values, -1, keepdims=True)
    centred = values - average
    variance = jnp.mean(centred * centred, -1, keepdims=True)
    return centred * lax.rsqrt(variance + 1e-06) * gain


def shards(activations, norm_gain, query_gain, key_gain, project_in, project_out):
    gathered_rows = lax.all_gather(activations, "tp", axis=1, tiled=True)
    normed = layer_norm(gathered_rows.astype(jnp.float32), norm_gain).astype(jnp.bfloat16)
    tok_rows = normed.shape[0]
    local_heads = project_in.shape[1]
    head_dim = project_in.shape[2] // 3
    piece = lax.all_gather(project_in, "rep", axis=0, tiled=True)
    running = jnp.dot(normed, piece.reshape(piece.shape[0], -1), preferred_element_type=jnp.float32)
    projected = running
    images_here = tok_rows // PATCHES
    projected = projected.reshape(images_here, PATCHES, local_heads, 3 * head_dim)
    queries = layer_norm(projected[..., :head_dim], query_gain).astype(jnp.bfloat16)
    keys_normed = layer_norm(projected[..., head_dim : 2 * head_dim], key_gain).astype(jnp.bfloat16)
    values = projected[..., 2 * head_dim :].astype(jnp.bfloat16)
    scores = jnp.einsum(
        "iphd,iqhd->ihpq", queries, keys_normed, preferred_element_type=jnp.float32
    ) / math.sqrt(head_dim)
    probabilities = jax.nn.softmax(scores, axis=-1).astype(jnp.bfloat16)
    mixed = jnp.einsum("ihpq,iqhd->iphd", probabilities, values, preferred_element_type=jnp.float32)
    mixed = mixed.astype(jnp.bfloat16).reshape(tok_rows, local_heads * head_dim)
    product = lax.dot_general(
        mixed,
        lax.all_gather(project_out, "rep", axis=0, tiled=True),
        (((1,), (1,)), ((), ())),
        preferred_element_type=jnp.float32,
    )
    attended = lax.psum_scatter(product.astype(jnp.bfloat16), "tp", scatter_dimension=1, tiled=True)
    local_in = jnp.sum(jnp.square(project_in.astype(jnp.float32)))
    local_out = jnp.sum(jnp.square(project_out.astype(jnp.float32)))
    total_in, total_out = lax.psum((local_in, local_out), ("rep", "tp"))
    weight_norms = jnp.stack([jnp.sqrt(total_in / (3 * HEADS * HEAD_DIM)), jnp.sqrt(total_out / D)])
    return (attended, weight_norms)


def solution(mesh):
    in_specs = (P("rep", "tp"), P(), P(), P(), P("rep", "tp", None), P("rep", "tp"))
    out_specs = (P("rep", "tp"), P())
    return jax.shard_map(shards, mesh=mesh, in_specs=in_specs, out_specs=out_specs, check_vma=False)
```

profile of v0, /device:TPU:0, one launch (start us, length us, event | category | flops | bytes accessed | tf_op | source)
XLA Modules:
  0.0 571.8 jit_solution(6341764529476445264)
XLA Ops:
  7.2 0.0 all-gather.4.cloned.1.call-start
  7.2 0.7 all-gather.4.cloned.1.call-update
  7.9 0.0 all-gather.6.cloned.1.call-start
  7.9 6.0 %copy.10 = bf16[384,12,384]{0,2,1:T(8,128)(2,1)} copy(bf16[384,12,384]{2,0,1:T(8,128)(2,1)} %param.10) | data formatting | bytes 7077888 | tf_op args[4]
  14.0 0.0 all-gather.6.cloned.1.call-update
  14.0 0.0 all-gather.8.cloned.1.call-start
  14.1 0.0 copy-start.3
  14.1 0.7 all-gather.8.cloned.1.call-update
  14.7 0.0 reduce-scatter.2.cloned.1.call-start
  14.8 77.8 %all-gather.4.cloned.1.call-done = bf16[512,6144]{1,0:T(8,128)(2,1)} async-done(((bf16[512,3072]{1,0:T(8,128)(2,1)}), bf16[512,6144]{1,0:T(8,128)(2,1)}) %all-gather.4.cloned.1.call-update) | async-done | bytes 6291472 | tf_op jit(solution)/shard_map/all_gather | solution.py:21
  92.6 3.8 convert_reduce_fusion
  96.5 0.7 copy-done
  97.2 1.8 fusion.5
  99.0 6.3 %fusion.7 = bf16[512,6144]{1,0:T(8,128)(2,1)} fusion(bf16[512,6144]{1,0:T(8,128)(2,1)S(1)} %copy-done, f32[6144]{0:T(1024)S(1)} %copy-done.3, f32[512]{0:T(512)S(1)} %add_rsqrt_fusion.2, f32[512]{0:T(512)S(1)} %broadcast_multiply_fusion.2), kind=kLoop, calls=%fused_computation.9 | loop fusion | flops 15728640 | bytes 12611584 | tf_op jit(solution)/shard_map/convert_element_type | solution.py:22
  105.3 265.2 %all-gather.6.cloned.1.call-done = bf16[6144,12,384]{0,2,1:T(8,128)(2,1)} async-done(((bf16[384,12,384]{0,2,1:T(8,128)(2,1)}), bf16[6144,12,384]{0,2,1:T(8,128)(2,1)}) %all-gather.6.cloned.1.call-update) | async-done | bytes 56623120 | tf_op jit(solution)/shard_map/all_gather | solution.py:26
  370.5 37.1 %fusion.1 = f32[2,256,12,384]{3,1,2,0:T(8,128)} fusion(bf16[2,256,6144,1]{2,1,3,0:T(8,128)(2,1)} %bitcast.26, bf16[6144,12,384]{0,2,1:T(8,128)(2,1)} %all-gather.6.cloned.1.call-done), kind=kOutput, calls=%fused_computation.1 | convolution fusion | flops 28991029248 | bytes 72351744 | tf_op jit(solution)/shard_map/dot_general | solution.py:27
  407.6 4.7 slice_reduce_fusion.1
  412.4 5.8 %multiply_reduce_fusion.3 = (f32[2,256,12]{1,2,0:T(8,128)S(1)}, f32[2,256,12]{1,2,0:T(8,128)S(1)}) fusion(f32[2,256,12,384]{3,1,2,0:T(8,128)} %fusion.1, f32[2,256,12]{1,2,0:T(8,128)S(1)} %get-tuple-element.11, f32[2,256,12]{1,2,0:T(8,128)S(1)} %get-tuple-element.10), kind=kLoop, calls=%fused_computation.21 | loop fusion | flops 4706304 | bytes 6389760 | tf_op jit(solution)/shard_map/reduce_sum | solution.py:16
  418.3 3.5 fusion.14
  421.8 5.0 fusion.23
  426.8 0.9 fusion.21
  427.7 1.6 copy.13
  429.3 0.3 copy.17
  429.7 41.3 %all-gather.8.cloned.1.call-done = bf16[6144,1536]{1,0:T(8,128)(2,1)} async-done(((bf16[384,1536]{1,0:T(8,128)(2,1)}), bf16[6144,1536]{1,0:T(8,128)(2,1)}) %all-gather.8.cloned.1.call-update) | async-done | bytes 18874384 | tf_op jit(solution)/shard_map/all_gather | solution.py:42
  471.0 15.6 %convolution_convert_fusion = bf16[512,6144]{1,0:T(8,128)(2,1)} fusion(bf16[512,1536]{0,1:T(8,128)(2,1)S(1)} %bitcast.28, bf16[6144,1536]{1,0:T(8,128)(2,1)} %all-gather.8.cloned.1.call-done), kind=kOutput, calls=%fused_computation.10 | convolution fusion | flops 9666822144 | bytes 26738688 | tf_op jit(solution)/shard_map/dot_general | solution.py:40
  486.6 0.0 reduce-scatter.2.cloned.1.call-update
  486.6 2.0 copy-done.2
  488.6 2.4 multiply_reduce_fusion
  491.0 2.5 multiply_reduce_fusion.4
  493.5 41.4 %all-reduce = (f32[]{:T(128)}, f32[]{:T(128)}) all-reduce(f32[]{:T(128)} %multiply_reduce_fusion.4, f32[]{:T(128)} %multiply_reduce_fusion), channel_id=1, replica_groups=mesh['rep'=16,'tp'=2] {'rep','tp'}, use_global_device_ids=true, to_apply=%region_12.0 | all-reduce | flops 2 | bytes 16 | tf_op jit(solution)/shard_map/psum | solution.py:49
  536.2 0.6 pad_maximum_fusion
  536.8 28.5 %reduce-scatter.2.cloned.1.call-done = bf16[512,3072]{1,0:T(8,128)(2,1)} async-done(((bf16[512,6144]{1,0:T(8,128)(2,1)}), bf16[512,3072]{1,0:T(8,128)(2,1)}) %reduce-scatter.2.cloned.1.call-update) | async-done | bytes 3145744 | tf_op jit(solution)/shard_map/reduce_scatter | solution.py:46
  (14 shorter events, 0.1 us)
Async XLA Ops:
  7.2 85.5 %all-gather.4.cloned.1.call-start = ((), (), s32[]{:S(2)}) async-start(), calls=%async_computation.1 | async-start | bytes 9437184 | tf_op jit(solution)/shard_map/all_gather | solution.py:21
  7.9 362.6 %all-gather.6.cloned.1.call-start = ((), (), s32[]{:S(2)}) async-start(), calls=%async_computation.2 | async-start | bytes 60162048 | tf_op jit(solution)/shard_map/all_gather | solution.py:26
  14.0 457.0 %all-gather.8.cloned.1.call-start = ((), (), s32[]{:S(2)}) async-start(), calls=%async_computation.3 | async-start | bytes 20054016 | tf_op jit(solution)/shard_map/all_gather | solution.py:42
  14.1 85.0 %copy-start.3 = (f32[6144]{0:T(1024)S(1)}, f32[6144]{0:T(1024)}, u32[]{:S(2)}) copy-start(f32[6144]{0:T(1024)} %param.7) | copy-start | bytes 73732
  14.7 550.6 %reduce-scatter.2.cloned.1.call-start = ((), (), s32[]{:S(2)}) async-start(), calls=%async_computation.4 | async-start | bytes 9437184 | tf_op jit(solution)/shard_map/reduce_scatter | solution.py:46
  92.6 4.6 copy-start
  407.6 10.6 %copy-start.1 = (f32[2,256,12,384]{3,1,2,0:T(8,128)S(1)}, f32[2,256,12,384]{3,1,2,0:T(8,128)}, u32[]{:S(2)}) copy-start(f32[2,256,12,384]{3,1,2,0:T(8,128)} %fusion.1) | copy-start | bytes 28311556
  407.6 10.6 %copy-start.4 = (f32[128]{0:T(128)S(1)}, f32[128]{0:T(128)}, u32[]{:S(2)}) copy-start(f32[128]{0:T(128)} %param.9) | copy-start | bytes 1540
  407.6 10.6 %copy-start.5 = (f32[128]{0:T(128)S(1)}, f32[128]{0:T(128)}, u32[]{:S(2)}) copy-start(f32[128]{0:T(128)} %param.8) | copy-start | bytes 1540
  486.6 2.0 copy-start.2
Sparse Core Ops, SparseCore 0:
  9.5 83.0 all-gather.3
  94.2 276.2 all-gather.5
  372.1 98.8 all-gather.7
  486.8 78.5 reduce-scatter.1
where the time goes:
time: 572 us
  waiting for transfers between devices  414 us (72%)
  matrix products  57.2 us (10%)
  blocking collectives  41.4 us (7%)
  other arithmetic  33 us (6%)
  between operations  15.2 us (3%)
  local copies, waits for them, and re-layouts  10.7 us (2%)
    all_gather x1, waiting for transfers between devices, shards(): piece = lax.all_gather(project_in, 'rep', axis=0, tiled=True)  265 us
    all_gather x1, waiting for transfers between devices, shards(): gathered_rows = lax.all_gather(activations, 'tp', axis=1, tiled=True)  77.8 us
    psum x1, blocking collectives, shards(): total_in, total_out = lax.psum((local_in, local_out), ('rep', 'tp'))  41.4 us
    all_gather x1, waiting for transfers between devices, shards(): lax.all_gather(project_out, 'rep', axis=0, tiled=True)  41.3 us
    dot_general x1, matrix products, shards(): jnp.dot(normed, piece.reshape(piece.shape[0], -1), preferred_element_type...  37.1 us
    reduce_scatter x1, waiting for transfers between devices, shards(): lax.psum_scatter(product.astype(jnp.bfloat16), 'tp', scatter_dimension=1,...  28.5 us
    dot_general x1, matrix products, shards(): lax.dot_general(mixed, lax.all_gather(project_out, 'rep', axis=0, tiled=T...  15.6 us
  transfers between devices with their start and end apart: 4, of which 4 were waited for; matrix products, arithmetic and copies ran while one was open for 14% of the time, Pallas kernels for 0%

commit v1 on v0

--- a/solution.py
+++ b/solution.py
@@ -23,7 +23,26 @@
     tok_rows = normed.shape[0]
     local_heads = project_in.shape[1]
     head_dim = project_in.shape[2] // 3
-    piece = lax.all_gather(project_in, "rep", axis=0, tiled=True)
+    size, index, extent = (lax.axis_size("rep"), lax.axis_index("rep"), project_in.shape[0])
+    forward = [(i, (i + 1) % size) for i in range(size)]
+    behind = [(i, (i - 1) % size) for i in range(size)]
+    out = jnp.zeros(
+        (*project_in.shape[:0], size * extent, *project_in.shape[0 + 1 :]), project_in.dtype
+    )
+    out = lax.dynamic_update_slice_in_dim(out, project_in, index * extent, axis=0)
+    from_left = from_right = project_in
+    half = size // 2
+    for turn in range(1, half + 1):
+        from_left = lax.ppermute(from_left, "rep", forward)
+        out = lax.dynamic_update_slice_in_dim(
+            out, from_left, (index - turn) % size * extent, axis=0
+        )
+        if turn < size - half:
+            from_right = lax.ppermute(from_right, "rep", behind)
+            out = lax.dynamic_update_slice_in_dim(
+                out, from_right, (index + turn) % size * extent, axis=0
+            )
+    piece = out
     running = jnp.dot(normed, piece.reshape(piece.shape[0], -1), preferred_element_type=jnp.float32)
     projected = running
     images_here = tok_rows // PATCHES

time: 572 us -> 860 us (1.50)
  starting transfers between devices: 0.16 us -> 526 us
  waiting for transfers between devices: 414 us -> 106 us
  local copies, waits for them, and re-layouts: 10.7 us -> 80 us
    ppermute x0 -> x15, starting transfers between devices: none -> 526 us  [the longest x8 517 us: shards(): from_left = lax.ppermute(from_left, 'rep', forward)]
    all_gather x1 -> x0, waiting for transfers between devices: 265 us -> none  [shards(): piece = lax.all_gather(project_in, 'rep', axis=0, tiled=True)]
    all_gather x1, waiting for transfers between devices: 77.8 us -> 0.01 us  [shards(): gathered_rows = lax.all_gather(activations, 'tp', axis=1, tiled=True)]
    ppermute x0 -> x15, waiting for transfers between devices: none -> 75.1 us  [the longest x8 75.1 us: shards(): from_left = lax.ppermute(from_left, 'rep', forward)]
    dynamic_update_slice x0 -> x16, local copies, waits for them, and re-layouts: none -> 51 us  [the longest x8 26.6 us: shards(): lax.dynamic_update_slice_in_dim(out, from_left, (index - turn) % size * e...]
    all_gather x1, waiting for transfers between devices: 41.3 us -> 0.02 us  [shards(): lax.all_gather(project_out, 'rep', axis=0, tiled=True)]
    broadcast_in_dim x0 -> x1, local copies, waits for them, and re-layouts: none -> 17.9 us  [shards(): jnp.zeros((*project_in.shape[:0], size * extent, *project_in.shape[0 + 1:...]
  transfers between devices with their start and end apart: 4 -> 18, of which waited for: 4 -> 8; matrix products, arithmetic and copies ran while one was open for 14% -> 17% of each run, Pallas kernels for 0% -> 0%
where the time goes in v1:
time: 860 us; the launch traced here: 859 us
  starting transfers between devices  526 us (61%)
  waiting for transfers between devices  106 us (12%)
  local copies, waits for them, and re-layouts  80 us (9%)
  matrix products  57.2 us (7%)
  blocking collectives  42.4 us (5%)
  other arithmetic  32.9 us (4%)
  between operations  15.3 us (2%)
    ppermute x8, starting transfers between devices, shards(): from_left = lax.ppermute(from_left, 'rep', forward)  517 us
    ppermute x8, waiting for transfers between devices, shards(): from_left = lax.ppermute(from_left, 'rep', forward)  75.1 us
    psum x1, blocking collectives, shards(): total_in, total_out = lax.psum((local_in, local_out), ('rep', 'tp'))  42.4 us
    dot_general x1, matrix products, shards(): jnp.dot(normed, piece.reshape(piece.shape[0], -1), preferred_element_type...  37.1 us
    reduce_scatter x1, waiting for transfers between devices, shards(): lax.psum_scatter(product.astype(jnp.bfloat16), 'tp', scatter_dimension=1,...  29.9 us
    dynamic_update_slice x8, local copies, waits for them, and re-layouts, shards(): lax.dynamic_update_slice_in_dim(out, from_left, (index - turn) % size * e...  26.6 us
    dynamic_update_slice x7, local copies, waits for them, and re-layouts, shards(): lax.dynamic_update_slice_in_dim(out, from_right, (index + turn) % size *...  22.1 us
    broadcast_in_dim x1, local copies, waits for them, and re-layouts, shards(): jnp.zeros((*project_in.shape[:0], size * extent, *project_in.shape[0 + 1:...  17.9 us
  transfers between devices with their start and end apart: 18, of which 8 were waited for; matrix products, arithmetic and copies ran while one was open for 17% of the time, Pallas kernels for 0%

profile of v1, /device:TPU:0, one launch (start us, length us, event | category | flops | bytes accessed | tf_op | source)
XLA Modules:
  0.0 859.4 jit_solution(12576278534395171416)
XLA Ops:
  7.9 4.6 copy.10
  13.0 5.0 collective-permute-start.1
  18.1 39.3 %collective-permute-done = bf16[384,12,384]{0,2,1:T(8,128)(2,1)} collective-permute-done((bf16[384,12,384]{0,2,1:T(8,128)(2,1)S(1)}, bf16[384,12,384]{0,2,1:T(8,128)(2,1)}, u32[]{:S(2)}, u32[]{:S(2)}) %collective-permute-start) | collective-permute-done | bytes 3538976 | tf_op jit(solution)/shard_map/ppermute | solution.py:36
  57.4 34.6 %collective-permute-start.2 = (bf16[384,12,384]{0,2,1:T(8,128)(2,1)}, bf16[384,12,384]{0,2,1:T(8,128)(2,1)}, u32[]{:S(2)}, u32[]{:S(2)}) collective-permute-start(bf16[384,12,384]{0,2,1:T(8,128)(2,1)} %collective-permute-done), channel_id=1, source_target_pairs={{0,2},{2,4},{4,6},{6,8},{8,10},{10,12},{12,14},{14,16},{16,18},{18... | collective-permute-start | bytes 10616840 | tf_op jit(solution)/shard_map/ppermute | solution.py:36
  92.2 9.3 %collective-permute-done.2 = bf16[384,12,384]{0,2,1:T(8,128)(2,1)} collective-permute-done((bf16[384,12,384]{0,2,1:T(8,128)(2,1)}, bf16[384,12,384]{0,2,1:T(8,128)(2,1)}, u32[]{:S(2)}, u32[]{:S(2)}) %collective-permute-start.2) | collective-permute-done | bytes 3538976 | tf_op jit(solution)/shard_map/ppermute | solution.py:36
  101.4 182.7 %collective-permute-start.4 = (bf16[384,12,384]{0,2,1:T(8,128)(2,1)}, bf16[384,12,384]{0,2,1:T(8,128)(2,1)S(1)}, u32[]{:S(2)}, u32[]{:S(2)}) collective-permute-start(bf16[384,12,384]{0,2,1:T(8,128)(2,1)} %collective-permute-done.2), channel_id=1, source_target_pairs={{0,2},{2,4},{4,6},{6,8},{8,10},{10,12},{12,14},{14,16},{16,18},{18... | collective-permute-start | bytes 10616840 | tf_op jit(solution)/shard_map/ppermute | solution.py:36
  285.8 4.7 collective-permute-done.4
  290.6 82.2 %collective-permute-start.6 = (bf16[384,12,384]{0,2,1:T(8,128)(2,1)S(1)}, bf16[384,12,384]{0,2,1:T(8,128)(2,1)S(1)}, u32[]{:S(2)}, u32[]{:S(2)}) collective-permute-start(bf16[384,12,384]{0,2,1:T(8,128)(2,1)S(1)} %collective-permute-done.4), channel_id=1, source_target_pairs={{0,2},{2,4},{4,6},{6,8},{8,10},{10,12},{12,14},{14,16},{16,18},{18... | collective-permute-start | bytes 10616840 | tf_op jit(solution)/shard_map/ppermute | solution.py:36
  372.8 5.8 collective-permute-done.6
  378.6 72.9 %collective-permute-start.8 = (bf16[384,12,384]{0,2,1:T(8,128)(2,1)S(1)}, bf16[384,12,384]{0,2,1:T(8,128)(2,1)S(1)}, u32[]{:S(2)}, u32[]{:S(2)}) collective-permute-start(bf16[384,12,384]{0,2,1:T(8,128)(2,1)S(1)} %collective-permute-done.6), channel_id=1, source_target_pairs={{0,2},{2,4},{4,6},{6,8},{8,10},{10,12},{12,14},{14,16},{16,18},{18... | collective-permute-start | bytes 10616840 | tf_op jit(solution)/shard_map/ppermute | solution.py:36
  451.6 5.8 collective-permute-done.8
  457.3 73.0 %collective-permute-start.10 = (bf16[384,12,384]{0,2,1:T(8,128)(2,1)S(1)}, bf16[384,12,384]{0,2,1:T(8,128)(2,1)}, u32[]{:S(2)}, u32[]{:S(2)}) collective-permute-start(bf16[384,12,384]{0,2,1:T(8,128)(2,1)S(1)} %collective-permute-done.8), channel_id=1, source_target_pairs={{0,2},{2,4},{4,6},{6,8},{8,10},{10,12},{12,14},{14,16},{16,18},{18... | collective-permute-start | bytes 10616840 | tf_op jit(solution)/shard_map/ppermute | solution.py:36
  530.3 6.0 collective-permute-done.10
  536.3 34.9 %collective-permute-start.12 = (bf16[384,12,384]{0,2,1:T(8,128)(2,1)}, bf16[384,12,384]{0,2,1:T(8,128)(2,1)}, u32[]{:S(2)}, u32[]{:S(2)}) collective-permute-start(bf16[384,12,384]{0,2,1:T(8,128)(2,1)} %collective-permute-done.10), channel_id=1, source_target_pairs={{0,2},{2,4},{4,6},{6,8},{8,10},{10,12},{12,14},{14,16},{16,18},{18... | collective-permute-start | bytes 10616840 | tf_op jit(solution)/shard_map/ppermute | solution.py:36
  571.2 17.9 %broadcast_in_dim.2 = bf16[6144,12,384]{0,2,1:T(8,128)(2,1)} broadcast(bf16[]{:T(256)} %constant.112.clone.1), dimensions={} | broadcast | bytes 56623104 | tf_op jit(solution)/shard_map/broadcast_in_dim | solution.py:29
  591.5 4.3 constant_dynamic-update-slice_fusion.14
  595.7 4.3 constant_dynamic-update-slice_fusion.13
  610.2 4.3 collective-permute-done.12
  614.4 36.0 %collective-permute-start.14 = (bf16[384,12,384]{0,2,1:T(8,128)(2,1)}, bf16[384,12,384]{0,2,1:T(8,128)(2,1)S(1)}, u32[]{:S(2)}, u32[]{:S(2)}) collective-permute-start(bf16[384,12,384]{0,2,1:T(8,128)(2,1)} %collective-permute-done.12), channel_id=1, source_target_pairs={{0,2},{2,4},{4,6},{6,8},{8,10},{10,12},{12,14},{14,16},{16,18},{18... | collective-permute-start | bytes 10616840 | tf_op jit(solution)/shard_map/ppermute | solution.py:36
  650.5 6.2 fusion.7
  656.7 4.5 constant_dynamic-update-slice_fusion.12
  674.7 4.4 constant_dynamic-update-slice_fusion.5
  679.0 4.5 constant_dynamic-update-slice_fusion.4
  683.5 4.4 constant_dynamic-update-slice_fusion.3
  687.8 4.4 constant_dynamic-update-slice_fusion.2
  696.9 37.1 %fusion.1 = f32[2,256,12,384]{3,1,2,0:T(8,128)} fusion(bf16[2,256,6144,1]{2,1,3,0:T(8,128)(2,1)} %bitcast.26, bf16[6144,12,384]{0,2,1:T(8,128)(2,1)} %constant_dynamic-update-slice_fusion), kind=kOutput, calls=%fused_computation.1 | convolution fusion | flops 28991029248 | bytes 72351744 | tf_op jit(solution)/shard_map/dot_general | solution.py:46
  734.1 4.7 slice_reduce_fusion.1
  738.8 5.7 multiply_reduce_fusion.3
  748.1 5.0 fusion.23
  756.0 15.6 %convolution_convert_fusion = bf16[512,6144]{1,0:T(8,128)(2,1)} fusion(bf16[512,1536]{0,1:T(8,128)(2,1)S(1)} %bitcast.28, bf16[6144,1536]{1,0:T(8,128)(2,1)} %all-gather.5.cloned.1.call-done), kind=kOutput, calls=%fused_computation.10 | convolution fusion | flops 9666822144 | bytes 26738688 | tf_op jit(solution)/shard_map/dot_general | solution.py:59
  778.6 42.4 %all-reduce = (f32[]{:T(128)}, f32[]{:T(128)}) all-reduce(f32[]{:T(128)} %multiply_reduce_fusion.4, f32[]{:T(128)} %multiply_reduce_fusion), channel_id=1, replica_groups=mesh['rep'=16,'tp'=2] {'rep','tp'}, use_global_device_ids=true, to_apply=%region_12.13 | all-reduce | flops 2 | bytes 16 | tf_op jit(solution)/shard_map/psum | solution.py:68
  822.9 29.9 %reduce-scatter.2.cloned.1.call-done = bf16[512,3072]{1,0:T(8,128)(2,1)} async-done(((bf16[512,6144]{1,0:T(8,128)(2,1)}), bf16[512,3072]{1,0:T(8,128)(2,1)}) %reduce-scatter.2.cloned.1.call-update) | async-done | bytes 3145744 | tf_op jit(solution)/shard_map/reduce_scatter | solution.py:65
  (82 shorter events, 47.9 us)
Async XLA Ops:
  7.2 592.8 %all-gather.3.cloned.1.call-start = ((), (), s32[]{:S(2)}) async-start(), calls=%async_computation.1 | async-start | bytes 9437184 | tf_op jit(solution)/shard_map/all_gather | solution.py:21
  7.9 748.1 %all-gather.5.cloned.1.call-start = ((), (), s32[]{:S(2)}) async-start(), calls=%async_computation.2 | async-start | bytes 20054016 | tf_op jit(solution)/shard_map/all_gather | solution.py:61
  12.5 44.9 %collective-permute-start = (bf16[384,12,384]{0,2,1:T(8,128)(2,1)S(1)}, bf16[384,12,384]{0,2,1:T(8,128)(2,1)}, u32[]{:S(2)}, u32[]{:S(2)}) collective-permute-start(bf16[384,12,384]{0,2,1:T(8,128)(2,1)S(1)} %copy.10), channel_id=1, source_target_pairs={{0,2},{2,4},{4,6},{6,8},{8,10},{10,12},{12,14},{14,16},{16,18},{18... | collective-permute-start | bytes 10616840 | tf_op jit(solution)/shard_map/ppermute | solution.py:36
  13.0 79.0 %collective-permute-start.1 = (bf16[384,12,384]{0,2,1:T(8,128)(2,1)S(1)}, bf16[384,12,384]{0,2,1:T(8,128)(2,1)}, u32[]{:S(2)}, u32[]{:S(2)}) collective-permute-start(bf16[384,12,384]{0,2,1:T(8,128)(2,1)S(1)} %copy.10), channel_id=1, source_target_pairs={{0,30},{2,0},{4,2},{6,4},{8,6},{10,8},{12,10},{14,12},{16,14},{18,... | collective-permute-start | bytes 10616840 | tf_op jit(solution)/shard_map/ppermute | solution.py:41
  57.4 44.0 %collective-permute-start.2 = (bf16[384,12,384]{0,2,1:T(8,128)(2,1)}, bf16[384,12,384]{0,2,1:T(8,128)(2,1)}, u32[]{:S(2)}, u32[]{:S(2)}) collective-permute-start(bf16[384,12,384]{0,2,1:T(8,128)(2,1)} %collective-permute-done), channel_id=1, source_target_pairs={{0,2},{2,4},{4,6},{6,8},{8,10},{10,12},{12,14},{14,16},{16,18},{18... | collective-permute-start | bytes 10616840 | tf_op jit(solution)/shard_map/ppermute | solution.py:36
  92.0 760.8 %reduce-scatter.2.cloned.1.call-start = ((), (), s32[]{:S(2)}) async-start(), calls=%async_computation.3 | async-start | bytes 9437184 | tf_op jit(solution)/shard_map/reduce_scatter | solution.py:65
  92.1 192.0 %collective-permute-start.3 = (bf16[384,12,384]{0,2,1:T(8,128)(2,1)}, bf16[384,12,384]{0,2,1:T(8,128)(2,1)S(1)}, u32[]{:S(2)}, u32[]{:S(2)}) collective-permute-start(bf16[384,12,384]{0,2,1:T(8,128)(2,1)} %collective-permute-done.1), channel_id=1, source_target_pairs={{0,30},{2,0},{4,2},{6,4},{8,6},{10,8},{12,10},{14,12},{16,14},{18,... | collective-permute-start | bytes 10616840 | tf_op jit(solution)/shard_map/ppermute | solution.py:41
  101.4 189.1 %collective-permute-start.4 = (bf16[384,12,384]{0,2,1:T(8,128)(2,1)}, bf16[384,12,384]{0,2,1:T(8,128)(2,1)S(1)}, u32[]{:S(2)}, u32[]{:S(2)}) collective-permute-start(bf16[384,12,384]{0,2,1:T(8,128)(2,1)} %collective-permute-done.2), channel_id=1, source_target_pairs={{0,2},{2,4},{4,6},{6,8},{8,10},{10,12},{12,14},{14,16},{16,18},{18... | collective-permute-start | bytes 10616840 | tf_op jit(solution)/shard_map/ppermute | solution.py:36
  285.8 86.9 %collective-permute-start.5 = (bf16[384,12,384]{0,2,1:T(8,128)(2,1)S(1)}, bf16[384,12,384]{0,2,1:T(8,128)(2,1)S(1)}, u32[]{:S(2)}, u32[]{:S(2)}) collective-permute-start(bf16[384,12,384]{0,2,1:T(8,128)(2,1)S(1)} %collective-permute-done.3), channel_id=1, source_target_pairs={{0,30},{2,0},{4,2},{6,4},{8,6},{10,8},{12,10},{14,12},{16,14},{18,... | collective-permute-start | bytes 10616840 | tf_op jit(solution)/shard_map/ppermute | solution.py:41
  290.6 82.2 %copy-start.5 = (bf16[384,12,384]{0,2,1:T(8,128)(2,1)}, bf16[384,12,384]{0,2,1:T(8,128)(2,1)S(1)}, u32[]{:S(2)}) copy-start(bf16[384,12,384]{0,2,1:T(8,128)(2,1)S(1)} %collective-permute-done.4) | copy-start | bytes 10616836
  290.6 88.0 %collective-permute-start.6 = (bf16[384,12,384]{0,2,1:T(8,128)(2,1)S(1)}, bf16[384,12,384]{0,2,1:T(8,128)(2,1)S(1)}, u32[]{:S(2)}, u32[]{:S(2)}) collective-permute-start(bf16[384,12,384]{0,2,1:T(8,128)(2,1)S(1)} %collective-permute-done.4), channel_id=1, source_target_pairs={{0,2},{2,4},{4,6},{6,8},{8,10},{10,12},{12,14},{14,16},{16,18},{18... | collective-permute-start | bytes 10616840 | tf_op jit(solution)/shard_map/ppermute | solution.py:36
  372.8 5.8 copy-start.7
  372.8 78.7 %collective-permute-start.7 = (bf16[384,12,384]{0,2,1:T(8,128)(2,1)S(1)}, bf16[384,12,384]{0,2,1:T(8,128)(2,1)S(1)}, u32[]{:S(2)}, u32[]{:S(2)}) collective-permute-start(bf16[384,12,384]{0,2,1:T(8,128)(2,1)S(1)} %collective-permute-done.5), channel_id=1, source_target_pairs={{0,30},{2,0},{4,2},{6,4},{8,6},{10,8},{12,10},{14,12},{16,14},{18,... | collective-permute-start | bytes 10616840 | tf_op jit(solution)/shard_map/ppermute | solution.py:41
  378.6 72.9 %copy-start.9 = (bf16[384,12,384]{0,2,1:T(8,128)(2,1)}, bf16[384,12,384]{0,2,1:T(8,128)(2,1)S(1)}, u32[]{:S(2)}) copy-start(bf16[384,12,384]{0,2,1:T(8,128)(2,1)S(1)} %collective-permute-done.6) | copy-start | bytes 10616836
  378.6 78.7 %collective-permute-start.8 = (bf16[384,12,384]{0,2,1:T(8,128)(2,1)S(1)}, bf16[384,12,384]{0,2,1:T(8,128)(2,1)S(1)}, u32[]{:S(2)}, u32[]{:S(2)}) collective-permute-start(bf16[384,12,384]{0,2,1:T(8,128)(2,1)S(1)} %collective-permute-done.6), channel_id=1, source_target_pairs={{0,2},{2,4},{4,6},{6,8},{8,10},{10,12},{12,14},{14,16},{16,18},{18... | collective-permute-start | bytes 10616840 | tf_op jit(solution)/shard_map/ppermute | solution.py:36
  451.5 5.8 copy-start.11
  451.5 78.8 %collective-permute-start.9 = (bf16[384,12,384]{0,2,1:T(8,128)(2,1)S(1)}, bf16[384,12,384]{0,2,1:T(8,128)(2,1)}, u32[]{:S(2)}, u32[]{:S(2)}) collective-permute-start(bf16[384,12,384]{0,2,1:T(8,128)(2,1)S(1)} %collective-permute-done.7), channel_id=1, source_target_pairs={{0,30},{2,0},{4,2},{6,4},{8,6},{10,8},{12,10},{14,12},{16,14},{18,... | collective-permute-start | bytes 10616840 | tf_op jit(solution)/shard_map/ppermute | solution.py:41
  457.3 73.0 %copy-start.13 = (bf16[384,12,384]{0,2,1:T(8,128)(2,1)}, bf16[384,12,384]{0,2,1:T(8,128)(2,1)S(1)}, u32[]{:S(2)}) copy-start(bf16[384,12,384]{0,2,1:T(8,128)(2,1)S(1)} %collective-permute-done.8) | copy-start | bytes 10616836
  457.3 79.0 %collective-permute-start.10 = (bf16[384,12,384]{0,2,1:T(8,128)(2,1)S(1)}, bf16[384,12,384]{0,2,1:T(8,128)(2,1)}, u32[]{:S(2)}, u32[]{:S(2)}) collective-permute-start(bf16[384,12,384]{0,2,1:T(8,128)(2,1)S(1)} %collective-permute-done.8), channel_id=1, source_target_pairs={{0,2},{2,4},{4,6},{6,8},{8,10},{10,12},{12,14},{14,16},{16,18},{18... | collective-permute-start | bytes 10616840 | tf_op jit(solution)/shard_map/ppermute | solution.py:36
  530.3 76.0 %collective-permute-start.11 = (bf16[384,12,384]{0,2,1:T(8,128)(2,1)}, bf16[384,12,384]{0,2,1:T(8,128)(2,1)}, u32[]{:S(2)}, u32[]{:S(2)}) collective-permute-start(bf16[384,12,384]{0,2,1:T(8,128)(2,1)} %collective-permute-done.9), channel_id=1, source_target_pairs={{0,30},{2,0},{4,2},{6,4},{8,6},{10,8},{12,10},{14,12},{16,14},{18,... | collective-permute-start | bytes 10616840 | tf_op jit(solution)/shard_map/ppermute | solution.py:41
  536.3 78.1 %collective-permute-start.12 = (bf16[384,12,384]{0,2,1:T(8,128)(2,1)}, bf16[384,12,384]{0,2,1:T(8,128)(2,1)}, u32[]{:S(2)}, u32[]{:S(2)}) collective-permute-start(bf16[384,12,384]{0,2,1:T(8,128)(2,1)} %collective-permute-done.10), channel_id=1, source_target_pairs={{0,2},{2,4},{4,6},{6,8},{8,10},{10,12},{12,14},{14,16},{16,18},{18... | collective-permute-start | bytes 10616840 | tf_op jit(solution)/shard_map/ppermute | solution.py:36
  600.0 4.6 copy-start
  600.0 50.5 %copy-start.15 = (f32[6144]{0:T(1024)S(1)}, f32[6144]{0:T(1024)}, u32[]{:S(2)}) copy-start(f32[6144]{0:T(1024)} %param.7) | copy-start | bytes 73732
  606.4 85.8 %collective-permute-start.13 = (bf16[384,12,384]{0,2,1:T(8,128)(2,1)}, bf16[384,12,384]{0,2,1:T(8,128)(2,1)S(1)}, u32[]{:S(2)}, u32[]{:S(2)}) collective-permute-start(bf16[384,12,384]{0,2,1:T(8,128)(2,1)} %collective-permute-done.11), channel_id=1, source_target_pairs={{0,30},{2,0},{4,2},{6,4},{8,6},{10,8},{12,10},{14,12},{16,14},{18,... | collective-permute-start | bytes 10616840 | tf_op jit(solution)/shard_map/ppermute | solution.py:41
  614.4 80.2 %collective-permute-start.14 = (bf16[384,12,384]{0,2,1:T(8,128)(2,1)}, bf16[384,12,384]{0,2,1:T(8,128)(2,1)S(1)}, u32[]{:S(2)}, u32[]{:S(2)}) collective-permute-start(bf16[384,12,384]{0,2,1:T(8,128)(2,1)} %collective-permute-done.12), channel_id=1, source_target_pairs={{0,2},{2,4},{4,6},{6,8},{8,10},{10,12},{12,14},{14,16},{16,18},{18... | collective-permute-start | bytes 10616840 | tf_op jit(solution)/shard_map/ppermute | solution.py:36
  656.7 4.6 copy-start.4
  656.7 6.7 copy-start.6
  663.5 4.5 copy-start.10
  668.0 4.5 copy-start.14
  734.0 10.5 %copy-start.1 = (f32[2,256,12,384]{3,1,2,0:T(8,128)S(1)}, f32[2,256,12,384]{3,1,2,0:T(8,128)}, u32[]{:S(2)}) copy-start(f32[2,256,12,384]{3,1,2,0:T(8,128)} %fusion.1) | copy-start | bytes 28311556
  734.0 10.5 %copy-start.16 = (f32[128]{0:T(128)S(1)}, f32[128]{0:T(128)}, u32[]{:S(2)}) copy-start(f32[128]{0:T(128)} %param.9) | copy-start | bytes 1540
  734.0 10.5 %copy-start.17 = (f32[128]{0:T(128)S(1)}, f32[128]{0:T(128)}, u32[]{:S(2)}) copy-start(f32[128]{0:T(128)} %param.8) | copy-start | bytes 1540
  (4 other events, 12.7 us)
Sparse Core Ops, SparseCore 0:
  9.5 83.0 all-gather.2
  94.2 245.2 all-gather.4
  771.8 80.9 reduce-scatter.1
